TPU v7x, 32 devices: a whole 2x2x4 slice. The times are simulated.
32 devices in a mesh: dp: 16 (over z, y, x), seq: 2 (over core).
Axes of the slice: x: 2, y: 2, z: 4, core: 2. Of those that a mesh axis runs over, the one named last changes fastest.
Arguments:
- activations: bfloat16 [4096, 8192], P(('dp', 'seq')), may hold values from -6 to 6
- queries: bfloat16 [4096, 8192], P(('dp', 'seq')), may hold values from -180 to 180
- keys: bfloat16 [4096, 1024], P(('dp', 'seq')), may hold values from -6 to 6
- out_grad: bfloat16 [4096, 8192], P(('dp', 'seq')), may hold values from -0.078125 to 0.078125
- layout: int32 [8192], replicated, may hold values from 0 to 8191, each once
Outputs:
- value_weight_grad: float32 [8192, 1024], P(('dp', 'seq'))
Inputs may be any that keep to these rules, and one draw needn't show every extreme that they name: `layout`: every row number 0 to 8191 appears exactly once.
All inputs are finite; a program needn't handle non-finite values.
Results may differ from a plain program's by a relative error of at most 0.0049.
Values may be sent and summed in bfloat16 or wider, within the bound.
A program may use at most 128 MiB of HBM per device.

v0:
```python
import jax
import jax.numpy as jnp
from jax import lax
from jax.sharding import PartitionSpec as P

H = 64
KVH = 8
HD = 128


def passed_along(value, axis, steps):
    count = lax.axis_size(axis)
    initial, last = (max(0, -steps), min(count, count - steps))
    return lax.ppermute(value, axis, [(source, source + steps) for source in range(initial, last)])


def local_values(queries, both_keys, out_grad, allowed):
    rows_here = queries.shape[0]
    per_group = H // KVH
    inv_root = 1.0 / float(HD) ** 0.5
    pieces = []
    for group_index in range(KVH):
        offset = group_index * per_group * HD
        query_block = queries[:, offset : offset + per_group * HD].reshape(rows_here, per_group, HD)
        grad_block = out_grad[:, offset : offset + per_group * HD].reshape(rows_here, per_group, HD)
        key_block = both_keys[:, group_index * HD : (group_index + 1) * HD]
        scores = (
            jnp.einsum("igd,jd->gij", query_block, key_block, preferred_element_type=jnp.float32)
            * inv_root
        )
        scores = jnp.where(allowed[None], scores, -jnp.inf)
        weights = jax.nn.softmax(scores, axis=-1).astype(jnp.bfloat16)
        pieces.append(
            jnp.einsum("gij,igd->jd", weights, grad_block, preferred_element_type=jnp.float32)
        )
    return jnp.concatenate(pieces, axis=1)


def rounded(term):
    return lax.optimization_barrier(term.astype(jnp.bfloat16)).astype(jnp.float32)


def body(activations, queries, keys, out_grad, layout):
    rows_here = activations.shape[0]
    seq_index = lax.axis_index("seq")
    earlier = passed_along(keys, "seq", 1)
    both_keys = jnp.concatenate([earlier, keys], axis=0)
    query_place = seq_index * rows_here + jnp.arange(rows_here)
    key_place = (seq_index - 1) * rows_here + jnp.arange(2 * rows_here)
    allowed = (key_place[None, :] <= query_place[:, None]) & (key_place[None, :] >= 0)
    partial_value = local_values(queries, both_keys, out_grad, allowed)
    returned = passed_along(partial_value[:rows_here], "seq", -1)
    value_grad = (partial_value[rows_here:] + returned).astype(jnp.bfloat16)
    model_width = activations.shape[1]
    dp_count = lax.axis_size("dp")
    seq_count = lax.axis_size("seq")
    owner_rows = model_width // (dp_count * seq_count)
    pair_rows, pair_grads = (
        lax.all_gather(activations, "seq", axis=0, tiled=True),
        lax.all_gather(value_grad, "seq", axis=0, tiled=True),
    )
    virtual = jnp.arange(lax.axis_size("dp") * owner_rows)
    buffer_rows = (
        virtual // owner_rows * (seq_count * owner_rows)
        + seq_index * owner_rows
        + virtual % owner_rows
    )
    columns = jnp.take(pair_rows, jnp.take(layout, buffer_rows), axis=1)
    return lax.psum_scatter(
        rounded(jnp.einsum("tr,tc->rc", columns, pair_grads, preferred_element_type=jnp.float32)),
        "dp",
        scatter_dimension=0,
        tiled=True,
    )


def solution(mesh):
    return jax.shard_map(
        body,
        mesh=mesh,
        in_specs=(
            P(("dp", "seq"), None),
            P(("dp", "seq"), None),
            P(("dp", "seq"), None),
            P(("dp", "seq"), None),
            P(),
        ),
        out_specs=P(("dp", "seq"), None),
        check_vma=False,
    )
```

profile of v0, /device:TPU:0, one launch (start us, length us, event | category | flops | bytes accessed | tf_op | source)
XLA Modules:
  0.0 473.0 jit_solution(6590788957329391209)
XLA Ops:
  6.5 3.2 collective-permute-start
  9.8 4.1 copy.23
  14.0 1.4 copy-done.1
  15.5 1.0 fusion.98
  16.5 0.9 copy-done.2
  17.6 1.8 copy.79
  19.4 1.8 copy.78
  21.1 1.8 copy.77
  27.7 0.9 copy.38
  28.6 0.9 copy.34
  32.0 23.0 %gather_fusion = s32[4096]{0:T(1024)S(1)} fusion(s32[8192]{0:T(1024)S(1)} %copy-done, s32[4096]{0:T(1024)S(1)} %broadcast_clamp_fusion.1), kind=kCustom, calls=%fused_computation | custom fusion | bytes 49152 | tf_op jit(solution)/shard_map/jit(_take)/gather | solution.py:68
  55.2 1.0 constant_dynamic-update-slice_fusion.1
  56.6 1.3 fusion.41
  61.0 1.4 fusion.104
  62.4 1.4 fusion.103
  63.8 2.8 fusion.49
  66.6 2.0 fusion.48
  68.6 2.1 fusion.47
  71.0 1.1 fusion.46
  72.3 1.1 fusion.45
  73.7 1.1 fusion.44
  75.1 1.1 fusion.43
  76.4 1.1 fusion.42
  77.5 1.1 slice.117
  78.6 1.3 collective-permute-start.1
  80.0 2.4 collective-permute-done.1
  82.4 1.1 fusion.51
  83.5 2.4 all_gather.7
  85.9 15.7 %gather_fusion.1 = bf16[4096,256]{1,0:T(8,128)(2,1)S(1)} fusion(bf16[256,8192]{0,1:T(8,128)(2,1)} %all-gather.2.cloned.1.call-done, s32[4096]{0:T(1024)S(1)} %broadcast_clamp_fusion), kind=kCustom, calls=%fused_computation.1 | custom fusion | bytes 4210688 | tf_op jit(solution)/shard_map/jit(_take)/gather | solution.py:68
  101.6 4.6 convolution_convert_fusion
  106.2 11.3 %convert_element_type.43 = f32[4096,1024]{1,0:T(8,128)} convert(bf16[4096,1024]{1,0:T(8,128)(2,1)} %convolution_convert_fusion) | non-fusion elementwise | flops 4194304 | bytes 25165824 | tf_op jit(solution)/shard_map/convert_element_type | solution.py:40
  117.5 348.7 %reduce-scatter.2.cloned.1.call-done = f32[256,1024]{1,0:T(8,128)} async-done(((f32[4096,1024]{1,0:T(8,128)}), f32[256,1024]{1,0:T(8,128)}) %reduce-scatter.2.cloned.1.call-update) | async-done | bytes 1048592 | tf_op jit(solution)/shard_map/reduce_scatter | solution.py:69
  (67 shorter events, 12.8 us)
Async XLA Ops:
  6.5 25.5 %copy-start = (s32[8192]{0:T(1024)S(1)}, s32[8192]{0:T(1024)}, u32[]{:S(2)}) copy-start(s32[8192]{0:T(1024)} %param.9) | copy-start | bytes 98308
  6.5 79.4 %all-gather.2.cloned.1.call-start = ((), (), s32[]{:S(2)}) async-start(), calls=%async_computation.1 | async-start | bytes 6291456 | tf_op jit(solution)/shard_map/all_gather | solution.py:59
  6.5 48.6 %collective-permute-start = (bf16[128,1024]{1,0:T(8,128)(2,1)}, bf16[128,1024]{1,0:T(8,128)(2,1)}, u32[]{:S(2)}, u32[]{:S(2)}) collective-permute-start(bf16[128,1024]{1,0:T(8,128)(2,1)} %param.7), channel_id=1, source_target_pairs={{0,1},{2,3},{4,5},{6,7},{8,9},{10,11},{12,13},{14,15},{16,17},{18,... | collective-permute-start | bytes 786440 | tf_op jit(solution)/shard_map/ppermute | solution.py:14
  13.9 1.6 copy-start.1
  13.9 452.3 %reduce-scatter.2.cloned.1.call-start = ((), (), s32[]{:S(2)}) async-start(), calls=%async_computation.2 | async-start | bytes 17825792 | tf_op jit(solution)/shard_map/reduce_scatter | solution.py:69
  15.5 1.9 copy-start.2
  32.0 24.2 %copy-start.8 = (bf16[128,1024]{1,0:T(8,128)(2,1)S(1)}, bf16[128,1024]{1,0:T(8,128)(2,1)}, u32[]{:S(2)}) copy-start(bf16[128,1024]{1,0:T(8,128)(2,1)} %param.7) | copy-start | bytes 786436
  58.3 1.1 copy-start.3
  59.1 1.0 copy-start.4
  59.4 1.1 copy-start.5
  68.6 2.1 copy-start.7
  68.6 2.4 copy-start.13
  70.9 1.1 copy-start.6
  70.9 1.4 copy-start.12
  72.3 1.4 copy-start.10
  73.7 1.4 copy-start.11
  75.1 1.4 copy-start.9
  78.6 3.8 collective-permute-start.1
Sparse Core Ops, SparseCore 0:
  14.0 14.8 all-gather.1
  117.6 348.4 reduce-scatter.1
where the time goes:
time: 478 us; the launch traced here: 473 us
  waiting for transfers between devices  351 us (73%)
  local copies, waits for them, and re-layouts  63 us (13%)
  matrix products  25.5 us (5%)
  between operations  13.7 us (3%)
  other arithmetic  12.7 us (3%)
    reduce_scatter x1, waiting for transfers between devices, body(): lax.psum_scatter(rounded(jnp.einsum('tr,tc->rc', columns, pair_grads, pre...  349 us
    gather x2, local copies, waits for them, and re-layouts, body(): columns = jnp.take(pair_rows, jnp.take(layout, buffer_rows), axis=1)  38.7 us
    unnamed x38, local copies, waits for them, and re-layouts  15.2 us
    dot_general x8, matrix products, local_values(): jnp.einsum('gij,igd->jd', weights, grad_block, preferred_element_type=jnp...  12.2 us
    convert_element_type x1, other arithmetic, rounded(): lax.optimization_barrier(term.astype(jnp.bfloat16)).astype(jnp.float32)  11.3 us
  transfers between devices with their start and end apart: 4, of which 2 were waited for; matrix products, arithmetic and copies ran while one was open for 14% of the time, Pallas kernels for 0%

commit v1 on v0

v1 whole, which is shorter than its diff:
```python
import functools

import jax
import jax.numpy as jnp
from jax import lax
from jax.experimental import pallas as pl
from jax.experimental.pallas import tpu as pltpu
from jax.sharding import PartitionSpec as P

H = 64
KVH = 8
HD = 128
AXES = ("dp", "seq")


def passed_along(value, axis, steps):
    count = lax.axis_size(axis)
    initial, last = (max(0, -steps), min(count, count - steps))
    return lax.ppermute(value, axis, [(source, source + steps) for source in range(initial, last)])


def gather_kernel(layout_ref, act_ref, out_ref, flipped, picked):
    width = act_ref.shape[1]
    step = 512

    def flip(i, carry):
        at = pl.multiple_of(i * step, step)
        flipped[pl.ds(at, step), :] = act_ref[:, pl.ds(at, step)].astype(jnp.float32).T
        return carry

    lax.fori_loop(0, width // step, flip, 0)
    rows = 256

    def pick(i, carry):
        at = pl.multiple_of(i * rows, rows)

        def some(j, inner):
            first = pl.multiple_of(j * 32, 32)
            for k in range(32):
                picked[pl.ds(first + k, 1), :] = flipped[pl.ds(layout_ref[at + first + k], 1), :]
            return inner

        lax.fori_loop(0, rows // 32, some, 0)
        out_ref[pl.ds(at, rows), :] = picked[...].astype(jnp.bfloat16)
        return carry

    lax.fori_loop(0, width // rows, pick, 0)


def gathered(activations, layout):
    tokens, width = activations.shape
    return pl.pallas_call(
        gather_kernel,
        out_shape=jax.ShapeDtypeStruct((width, tokens), jnp.bfloat16),
        in_specs=[
            pl.BlockSpec(memory_space=pltpu.SMEM),
            pl.BlockSpec(memory_space=pltpu.VMEM),
        ],
        out_specs=pl.BlockSpec(memory_space=pltpu.VMEM),
        scratch_shapes=[
            pltpu.VMEM((width, tokens), jnp.float32),
            pltpu.VMEM((256, tokens), jnp.float32),
        ],
        cost_estimate=pl.CostEstimate(flops=10**7, bytes_accessed=2 * 2**20, transcendentals=0),
    )(layout, activations)


def attention_kernel(q_ref, early_ref, keys_ref, grad_ref, out_ref, *, per_group):
    tokens = q_ref.shape[0]
    seq_index = lax.axis_index("seq")
    both_keys = jnp.concatenate([early_ref[...], keys_ref[...]], axis=0)
    place = lax.broadcasted_iota(jnp.int32, (tokens, 2 * tokens), 0)
    other = lax.broadcasted_iota(jnp.int32, (tokens, 2 * tokens), 1)
    allowed = (other <= place + tokens) & (other >= jnp.where(seq_index == 0, tokens, 0))
    total = jnp.zeros((2 * tokens, HD), jnp.float32)
    for head in range(per_group):
        columns = slice(head * HD, (head + 1) * HD)
        scores = lax.dot_general(
            q_ref[:, columns], both_keys, (((1,), (1,)), ((), ())),
            preferred_element_type=jnp.float32,
        ) * (1.0 / float(HD) ** 0.5)
        scores = jnp.where(allowed, scores, -jnp.inf)
        powers = jnp.exp(scores - jnp.max(scores, axis=1, keepdims=True))
        weights = (powers / jnp.sum(powers, axis=1, keepdims=True)).astype(jnp.bfloat16)
        total += lax.dot_general(
            weights, grad_ref[:, columns], (((0,), (0,)), ((), ())),
            preferred_element_type=jnp.float32,
        )
    out_ref[...] = total


def partial_values(queries, earlier, keys, out_grad):
    tokens = queries.shape[0]
    per_group = H // KVH
    wide = pl.BlockSpec((tokens, per_group * HD), lambda g: (0, g))
    narrow = pl.BlockSpec((tokens, HD), lambda g: (0, g))
    return pl.pallas_call(
        functools.partial(attention_kernel, per_group=per_group),
        grid=(KVH,),
        out_shape=jax.ShapeDtypeStruct((2 * tokens, KVH * HD), jnp.float32),
        in_specs=[wide, narrow, narrow, wide],
        out_specs=pl.BlockSpec((2 * tokens, HD), lambda g: (0, g)),
        cost_estimate=pl.CostEstimate(
            flops=8 * H * HD * tokens * tokens, bytes_accessed=6 * 2**20, transcendentals=2**21
        ),
    )(queries, earlier, keys, out_grad)


def body(activations, queries, keys, out_grad, layout):
    rows_here = activations.shape[0]
    devices = lax.axis_size("dp") * lax.axis_size("seq")
    columns = gathered(activations, layout)
    owned = lax.all_to_all(columns, AXES, 0, 0, tiled=True)
    earlier = passed_along(keys, "seq", 1)
    partial = partial_values(queries, earlier, keys, out_grad)
    returned = passed_along(partial[:rows_here], "seq", -1)
    value_grad = (partial[rows_here:] + returned).astype(jnp.bfloat16)
    values = lax.all_gather(value_grad, AXES, axis=0, tiled=True)
    owned = owned.reshape(devices, -1, rows_here)
    return jnp.einsum(
        "srt,stc->rc",
        owned,
        values.reshape(devices, rows_here, -1),
        preferred_element_type=jnp.float32,
    )


def solution(mesh):
    return jax.shard_map(
        body,
        mesh=mesh,
        in_specs=(P(AXES, None),) * 4 + (P(),),
        out_specs=P(AXES, None),
        check_vma=False,
    )
```

time: 478 us -> 145 us (0.30); the launches traced: 473 us -> 145 us
  waiting for transfers between devices: 351 us -> 6.38 us
  blocking collectives: 2.39 us -> 89.3 us
  local copies, waits for them, and re-layouts: 63 us -> 1.77 us
  Pallas kernels: 0 us -> 22.7 us
  matrix products: 25.5 us -> 5.69 us
  other arithmetic: 12.7 us -> 1.81 us
    reduce_scatter x1 -> x0, waiting for transfers between devices: 349 us -> none  [body(): lax.psum_scatter(rounded(jnp.einsum('tr,tc->rc', columns, pair_grads, pre...]
    all_to_all x0 -> x1, blocking collectives: none -> 89.3 us  [body(): owned = lax.all_to_all(columns, AXES, 0, 0, tiled=True)]
    gather x2 -> x0, local copies, waits for them, and re-layouts: 38.7 us -> none  [body(): columns = jnp.take(pair_rows, jnp.take(layout, buffer_rows), axis=1)]
    pallas_call x0 -> x2, Pallas kernels: none -> 22.7 us  [the longest x1 12.5 us: gathered(): pl.pallas_call(gather_kernel, out_shape=jax.ShapeDtypeStruct((width, toke...]
    unnamed x38 -> x2, local copies, waits for them, and re-layouts: 15.2 us -> 0.7 us
    dot_general x17 -> x1, matrix products: 20 us -> 5.69 us  [body(): jnp.einsum('srt,stc->rc', owned, values.reshape(devices, rows_here, -1),...]
    convert_element_type x2 -> x1, other arithmetic: 12.4 us -> 1.81 us  [body(): value_grad = (partial[rows_here:] + returned).astype(jnp.bfloat16)]
    slice x11 -> x1, local copies, waits for them, and re-layouts: 9.08 us -> 1.08 us  [body(): returned = passed_along(partial[:rows_here], 'seq', -1)]
  transfers between devices with their start and end apart: 4 -> 3, of which waited for: 2 -> 3; matrix products, arithmetic and copies ran while one was open for 14% -> 0% of each run, Pallas kernels for 0% -> 9%
where the time goes in v1:
time: 145 us
  blocking collectives  89.3 us (62%)
  Pallas kernels  22.7 us (16%)
  between operations  13.4 us (9%)
  waiting for transfers between devices  6.38 us (4%)
  matrix products  5.69 us (4%)
  starting transfers between devices  3.69 us (3%)
  other arithmetic  1.81 us (1%)
  local copies, waits for them, and re-layouts  1.77 us (1%)
    all_to_all x1, blocking collectives, body(): owned = lax.all_to_all(columns, AXES, 0, 0, tiled=True)  89.3 us
    pallas_call x1, Pallas kernels, gathered(): pl.pallas_call(gather_kernel, out_shape=jax.ShapeDtypeStruct((width, toke...  12.5 us
    pallas_call x1, Pallas kernels, partial_values(): pl.pallas_call(functools.partial(attention_kernel, per_group=per_group),...  10.3 us
    dot_general x1, matrix products, body(): jnp.einsum('srt,stc->rc', owned, values.reshape(devices, rows_here, -1),...  5.69 us
    ppermute x2, waiting for transfers between devices, passed_along(): lax.ppermute(value, axis, [(source, source + steps) for source in range(i...  3.84 us
    ppermute x2, starting transfers between devices, passed_along(): lax.ppermute(value, axis, [(source, source + steps) for source in range(i...  3.69 us
  transfers between devices with their start and end apart: 3, of which 3 were waited for; matrix products, arithmetic and copies ran while one was open for 0% of the time, Pallas kernels for 9%

profile of v1, /device:TPU:0, one launch (start us, length us, event | category | flops | bytes accessed | tf_op | source)
XLA Modules:
  0.0 144.8 jit_solution(16420719013003440419)
XLA Ops:
  6.5 0.0 all-gather.2.cloned.1.call-start
  6.5 2.4 %collective-permute-start = (bf16[128,1024]{1,0:T(8,128)(2,1)}, bf16[128,1024]{1,0:T(8,128)(2,1)S(1)}, u32[]{:S(2)}, u32[]{:S(2)}) collective-permute-start(bf16[128,1024]{1,0:T(8,128)(2,1)} %keys_ref.1), channel_id=1, source_target_pairs={{0,1},{2,3},{4,5},{6,7},{8,9},{10,11},{12,13},{14,15},{16,17},{18,... | collective-permute-start | bytes 786440 | tf_op jit(solution)/shard_map/ppermute | solution.py:19
  8.9 1.3 collective-permute-done.early_ref
  10.3 0.0 copy-start
  10.3 0.7 copy-done
  11.0 10.3 %shard_map.56 = f32[256,1024]{1,0:T(8,128)} custom-call(bf16[128,8192]{1,0:T(8,128)(2,1)} %q_ref.1, bf16[128,1024]{1,0:T(8,128)(2,1)} %copy-done, bf16[128,1024]{1,0:T(8,128)(2,1)} %keys_ref.1, bf16[128,8192]{1,0:T(8,128)(2,1)} %grad_ref.1), custom_call_target="tpu_custom_call" | custom-call | flops 1073741824 | bytes 6291456 | tf_op jit(solution)/shard_map/pallas_call | solution.py:97
  21.2 1.1 slice.9
  22.3 1.3 collective-permute-start.1
  23.6 2.5 %collective-permute-done.1 = f32[128,1024]{1,0:T(8,128)S(1)} collective-permute-done((f32[128,1024]{1,0:T(8,128)S(1)}, f32[128,1024]{1,0:T(8,128)S(1)}, u32[]{:S(2)}, u32[]{:S(2)}) %collective-permute-start.1) | collective-permute-done | bytes 524320 | tf_op jit(solution)/shard_map/ppermute | solution.py:19
  26.1 1.8 %fusion = bf16[128,1024]{1,0:T(8,128)(2,1)} fusion(f32[128,1024]{1,0:T(8,128)S(1)} %collective-permute-done.1, f32[256,1024]{1,0:T(8,128)} %shard_map.56), kind=kLoop, calls=%fused_computation.2 | loop fusion | flops 262144 | bytes 1310720 | tf_op jit(solution)/shard_map/convert_element_type | solution.py:117
  27.9 0.0 all-gather.2.cloned.1.call-update
  28.0 12.5 %shard_map.55 = bf16[8192,128]{1,0:T(8,128)(2,1)} custom-call(s32[8192]{0:T(1024)} %layout_ref.1, bf16[128,8192]{1,0:T(8,128)(2,1)} %act_ref.1), custom_call_target="tpu_custom_call" | custom-call | flops 10000000 | bytes 2097152 | tf_op jit(solution)/shard_map/pallas_call | solution.py:52
  40.4 89.3 %all_to_all.9 = bf16[32,256,128]{2,1,0:T(8,128)(2,1)S(1)} all-to-all(bf16[32,256,128]{2,1,0:T(8,128)(2,1)} %bitcast.6), channel_id=1, replica_groups=mesh['dp'=16,'seq'=2] {'dp','seq'}, dimensions={0} | all-to-all | bytes 4194304 | tf_op jit(solution)/shard_map/all_to_all | solution.py:113
  129.8 2.5 %all-gather.2.cloned.1.call-done = bf16[4096,1024]{1,0:T(8,128)(2,1)} async-done(((bf16[128,1024]{1,0:T(8,128)(2,1)}), bf16[4096,1024]{1,0:T(8,128)(2,1)}) %all-gather.2.cloned.1.call-update) | async-done | bytes 8388624 | tf_op jit(solution)/shard_map/all_gather | solution.py:118
  132.3 5.7 %convolution_bitcast_fusion = f32[256,1024]{1,0:T(8,128)} fusion(bf16[32,256,128]{2,1,0:T(8,128)(2,1)S(1)} %all_to_all.9, bf16[32,128,1024]{2,1,0:T(8,128)(2,1)} %bitcast.7), kind=kOutput, calls=%fused_computation | convolution fusion | flops 2147483648 | bytes 11534336 | tf_op jit(solution)/shard_map/srt,stc->rc/dot_general | solution.py:120
Async XLA Ops:
  6.5 125.7 %all-gather.2.cloned.1.call-start = ((), (), s32[]{:S(2)}) async-start(), calls=%async_computation.1 | async-start | bytes 8650752 | tf_op jit(solution)/shard_map/all_gather | solution.py:118
  6.5 3.7 %collective-permute-start = (bf16[128,1024]{1,0:T(8,128)(2,1)}, bf16[128,1024]{1,0:T(8,128)(2,1)S(1)}, u32[]{:S(2)}, u32[]{:S(2)}) collective-permute-start(bf16[128,1024]{1,0:T(8,128)(2,1)} %keys_ref.1), channel_id=1, source_target_pairs={{0,1},{2,3},{4,5},{6,7},{8,9},{10,11},{12,13},{14,15},{16,17},{18,... | collective-permute-start | bytes 786440 | tf_op jit(solution)/shard_map/ppermute | solution.py:19
  10.3 0.7 copy-start
  22.3 3.8 %collective-permute-start.1 = (f32[128,1024]{1,0:T(8,128)S(1)}, f32[128,1024]{1,0:T(8,128)S(1)}, u32[]{:S(2)}, u32[]{:S(2)}) collective-permute-start(f32[128,1024]{1,0:T(8,128)S(1)} %slice.9), channel_id=1, source_target_pairs={{1,0},{3,2},{5,4},{7,6},{9,8},{11,10},{13,12},{15,14},{17,16},{19,... | collective-permute-start | bytes 1572872 | tf_op jit(solution)/shard_map/ppermute | solution.py:19
Sparse Core Ops, SparseCore 0:
  28.1 104.1 all-gather.1
